TPU v7x, 256 devices: a whole 4x4x8 slice. The times are simulated.
256 devices in a mesh: rep: 32 (over y_hi, z, core), tp: 8 (over y_lo, x).
Axes of the slice: x: 4, y: 4 (y_hi: 2, y_lo: 2; y = y_hi * 2 + y_lo), z: 8, core: 2. Of those that a mesh axis runs over, the one named last changes fastest.
Arguments:
- queries: bfloat16 [8192, 8192], P('rep', 'tp'), may hold values from -8 to 8
- cand_keys: bfloat16 [8192, 1024], P('rep', 'tp'), may hold values from -6 to 6
- cand_values: bfloat16 [8192, 1024], P('rep', 'tp'), may hold values from -6 to 6
- prefix_kv: bfloat16 [32, 2, 4096, 1024], P('rep', None, None, 'tp'), may hold values from -8 to 8
- owner: int32 [1], replicated, may hold values from 0 to 31
- lengths: int32 [32, 2], P('rep'), may hold values from 1 to 128, as said below
- out_weight: bfloat16 [8192, 4096], P('tp'), may hold values from -2.390625 to 2.390625
Outputs:
- attn_out: bfloat16 [8192, 4096], P(('rep', 'tp'))
Inputs may be any that keep to these rules, and one draw needn't show every extreme that they name: Only the slice of prefix_kv at index owner[0] is read. Candidate c of group g has its real tokens in its first lengths[g, c] slots; the rest are padding.
All inputs are finite; a program needn't handle non-finite values.
Results may differ from a plain program's by a relative error of at most 0.017.
Values may be sent and summed in bfloat16 or wider, within the bound.
No kernel may reach another device: no remote copies, remote signals or barrier semaphores. Data moves between devices by JAX's collectives and lax.ppermute only.
A program may use at most 64 MiB of HBM per device.

v0:
```python
import math
import jax
import jax.numpy as jnp
from jax import lax
from jax.sharding import PartitionSpec as P

QH = 64
KVH = 8
HD = 128
CLEN = 128
NEG = -1e30


def padded_to(lines, count):
    spare = -len(lines) % count
    return jnp.pad(lines, [(0, spare)] + [(0, 0)] * (lines.ndim - 1))


def broadcast_by_parts(shard, axis, root):
    lines = jnp.where(lax.axis_index(axis) == root, shard, jnp.zeros_like(shard)).reshape(
        -1, *shard.shape[1:][-1:]
    )
    padded = padded_to(lines, lax.axis_size(axis))
    own = lax.psum_scatter(padded, axis, scatter_dimension=0, tiled=True)
    return lax.all_gather(own, axis, axis=0, tiled=True)[: len(lines)].reshape(shard.shape)


def split_up(shard, dim, count):
    before, after = (shard.shape[:dim], shard.shape[dim + 1 :])
    return jnp.moveaxis(shard.reshape(*before, count, -1, *after), dim, 0)


def summed_on_arrival(shard, axis, dim):
    count = lax.axis_size(axis)
    tiles = lax.all_to_all(split_up(shard, dim, count), axis, 0, 0, tiled=True)
    return jnp.sum(tiles.astype(jnp.float32), axis=0)


def body(queries, cand_keys, cand_values, prefix_kv, owner, lengths, out_weight):
    row_count = queries.shape[0]
    kv_heads = cand_keys.shape[1] // HD
    head_group = QH // KVH
    cand_count = row_count // CLEN
    score_scale = 1.0 / math.sqrt(HD)
    query_grid = queries.reshape(row_count, kv_heads, head_group, HD)
    cand_queries = queries.reshape(cand_count, CLEN, kv_heads, head_group, HD)
    key_grid = cand_keys.reshape(cand_count, CLEN, kv_heads, HD)
    value_grid = cand_values.reshape(cand_count, CLEN, kv_heads, HD)
    own_scores = (
        jnp.einsum("cikgd,cjkd->kgcij", cand_queries, key_grid, preferred_element_type=jnp.float32)
        * score_scale
    )
    live_mask = jnp.arange(CLEN, dtype=jnp.int32)[None, :] < lengths[0][:, None]
    own_scores = jnp.where(live_mask[None, None, :, None, :], own_scores, NEG)
    own_max = jnp.max(own_scores, -1)
    exponent = jnp.exp(own_scores - own_max[..., None])
    row_total = jnp.sum(exponent, -1).reshape(kv_heads, head_group, row_count)
    weighted = jnp.einsum(
        "kgcij,cjkd->kgcid",
        exponent.astype(jnp.bfloat16),
        value_grid,
        preferred_element_type=jnp.float32,
    )
    weighted = weighted.reshape(kv_heads, head_group, row_count, HD)
    row_max = own_max.reshape(kv_heads, head_group, row_count)

    def absorb(running, block_keys, block_values):
        old_max, old_total, old_weighted = running
        block_width = block_keys.shape[0]
        scores = (
            jnp.einsum(
                "xlpm,vlm->lpxv",
                query_grid,
                block_keys.reshape(block_width, kv_heads, HD),
                preferred_element_type=jnp.float32,
            )
            * score_scale
        )
        new_max = jnp.maximum(old_max, jnp.max(scores, -1))
        factor = jnp.exp(old_max - new_max)
        block_expo = jnp.exp(scores - new_max[..., None])
        new_total = old_total * factor + jnp.sum(block_expo, -1)
        new_weighted = old_weighted * factor[..., None] + jnp.einsum(
            "ipuo,oit->iput",
            block_expo.astype(jnp.bfloat16),
            block_values.reshape(block_width, kv_heads, HD),
            preferred_element_type=jnp.float32,
        )
        return (new_max, new_total, new_weighted)

    prefix_len = prefix_kv.shape[2]
    block_width = min(1024, prefix_len)
    block_count = prefix_len // block_width
    owner_index = owner[0]
    own_prefix = prefix_kv[0]
    arrived = broadcast_by_parts(own_prefix, "rep", owner_index)

    def advance(block_index, running):
        prefix_piece = lax.dynamic_slice_in_dim(arrived, block_index * block_width, block_width, 1)
        return absorb(running, prefix_piece[0], prefix_piece[1])

    row_max, row_total, weighted = lax.fori_loop(
        0, block_count, advance, (row_max, row_total, weighted)
    )
    context = weighted / row_total[..., None]
    context = (
        jnp.transpose(context, (2, 0, 1, 3))
        .reshape(row_count, kv_heads * head_group * HD)
        .astype(jnp.bfloat16)
    )
    summed = summed_on_arrival(
        jnp.dot(context, out_weight, preferred_element_type=jnp.float32).astype(jnp.bfloat16),
        "tp",
        0,
    )
    return summed.astype(jnp.bfloat16)


def solution(mesh):
    in_specs = (
        P("rep", "tp"),
        P("rep", "tp"),
        P("rep", "tp"),
        P("rep", None, None, "tp"),
        P(),
        P("rep", None),
        P("tp", None),
    )
    out_specs = P(("rep", "tp"), None)
    return jax.shard_map(body, mesh=mesh, in_specs=in_specs, out_specs=out_specs, check_vma=False)
```

profile of v0, /device:TPU:1, one launch (start us, length us, event | category | flops | bytes accessed | tf_op | source)
XLA Modules:
  0.0 312.3 jit_solution(9816006664559664985)
XLA Ops:
  6.5 0.0 copy-start
  6.5 0.0 copy-start.3
  6.5 0.0 copy-start.2
  6.5 0.0 reduce-scatter.2.cloned.1.call-start
  7.2 1.5 broadcast_select_fusion
  8.7 0.0 reduce-scatter.2.cloned.1.call-update
  8.8 0.0 all-gather.2.cloned.1.call-start
  8.8 121.0 %reduce-scatter.2.cloned.1.call-done = bf16[256,128]{1,0:T(8,128)(2,1)} async-done(((bf16[8192,128]{1,0:T(8,128)(2,1)}), bf16[256,128]{1,0:T(8,128)(2,1)}) %reduce-scatter.2.cloned.1.call-update) | async-done | bytes 65552 | tf_op jit(solution)/shard_map/reduce_scatter | solution.py:24
  129.8 0.0 all-gather.2.cloned.1.call-update
  129.8 1.2 copy.15
  131.1 1.1 copy.22
  132.2 0.0 copy-done.3
  132.2 0.1 iota_compare_fusion
  132.3 0.0 copy-done
  132.3 0.3 fusion.29
  132.6 0.0 copy-done.2
  132.7 0.4 convolution_bitcast_fusion
  133.0 0.1 copy.14
  133.1 0.3 copy.16
  133.4 0.2 fusion.24
  133.5 82.6 %all-gather.2.cloned.1.call-done = bf16[8192,128]{1,0:T(8,128)(2,1)} async-done(((bf16[256,128]{1,0:T(8,128)(2,1)}), bf16[8192,128]{1,0:T(8,128)(2,1)}) %all-gather.2.cloned.1.call-update) | async-done | bytes 2097168 | tf_op jit(solution)/shard_map/all_gather | solution.py:25
  216.2 51.1 %while.17 = (s32[]{:T(128)}, f32[1,8,256]{2,1,0:T(8,128)S(1)}, f32[1,8,256]{2,1,0:T(8,128)S(1)}, f32[1,8,256,128]{3,2,1,0:T(8,128)S(1)}, bf16[2,4096,128]{2,1,0:...) while((s32[]{:T(128)}, f32[1,8,256]{2,1,0:T(8,128)S(1)}, ...), condition=%wide.region_6.7_spmd, body=%wide.region_3.6_spmd.sunk | while | flops 1091049472 | bytes 61997260 | solution.py:102
  216.2 5.4 %bitcast_reduce_fusion.2 = (f32[8,256]{1,0:T(8,128)S(1)}, f32[1024,256,8]{1,0,2:T(8,128)}) fusion(bf16[256,1,8,128]{3,0,2,1:T(8,128)(2,1)S(1)} %get-tuple-element.213, bf16[2,4096,128]{2,1,0:T(8,128)(2,1)} %get-tuple-element.212, s32[]{:T(128)S(6)} %select_n.37), kind=kOutput, calls=%fused_computation.1.clone.1 | convolution fusion | flops 541063168 | bytes 9183236 | tf_op jit(solution)/shard_map/while/body/eval_jaxpr/xlpm,vlm->lpxv/dot_general | solution.py:71
  221.6 0.0 copy-start.1
  221.6 4.6 %fusion.41 = f32[1,8,256,128]{3,2,1,0:T(8,128)S(1)} fusion(f32[1024,256,8]{1,0,2:T(8,128)} %get-tuple-element.184, f32[8,256]{1,0:T(8,128)S(1)} %bitcast.126, f32[1,8,256,128]{3,2,1,0:T(8,128)S(1)} %get-tuple-element.200, f32[8,256]{1,0:T(8,128)S(1)} %get-tuple-element.185, bf16[2,4096,128]{2,1,0:T(8,128)(2,1)} %get-tuple-element.212, s32[]{:T(128)S(6)} %add.51, ...), kind=kOutput, calls=%fused_computation.10.clone.1 | convolution fusion | flops 543686656 | bytes 10764296 | tf_op jit(solution)/shard_map/while/body/eval_jaxpr/ipuo,oit->iput/dot_general | solution.py:83
  226.2 1.3 copy-done.1
  227.5 1.4 fusion.40
  228.9 5.4 %bitcast_reduce_fusion.2 = (f32[8,256]{1,0:T(8,128)S(1)}, f32[1024,256,8]{1,0,2:T(8,128)}) fusion(bf16[256,1,8,128]{3,0,2,1:T(8,128)(2,1)S(1)} %get-tuple-element.213, bf16[2,4096,128]{2,1,0:T(8,128)(2,1)} %get-tuple-element.212, s32[]{:T(128)S(6)} %select_n.37), kind=kOutput, calls=%fused_computation.1.clone.1 | convolution fusion | flops 541063168 | bytes 9183236 | tf_op jit(solution)/shard_map/while/body/eval_jaxpr/xlpm,vlm->lpxv/dot_general | solution.py:71
  234.4 0.0 copy-start.1
  234.4 4.6 %fusion.41 = f32[1,8,256,128]{3,2,1,0:T(8,128)S(1)} fusion(f32[1024,256,8]{1,0,2:T(8,128)} %get-tuple-element.184, f32[8,256]{1,0:T(8,128)S(1)} %bitcast.126, f32[1,8,256,128]{3,2,1,0:T(8,128)S(1)} %get-tuple-element.200, f32[8,256]{1,0:T(8,128)S(1)} %get-tuple-element.185, bf16[2,4096,128]{2,1,0:T(8,128)(2,1)} %get-tuple-element.212, s32[]{:T(128)S(6)} %add.51, ...), kind=kOutput, calls=%fused_computation.10.clone.1 | convolution fusion | flops 543686656 | bytes 10764296 | tf_op jit(solution)/shard_map/while/body/eval_jaxpr/ipuo,oit->iput/dot_general | solution.py:83
  239.0 1.3 copy-done.1
  240.3 1.4 fusion.40
  241.7 5.4 %bitcast_reduce_fusion.2 = (f32[8,256]{1,0:T(8,128)S(1)}, f32[1024,256,8]{1,0,2:T(8,128)}) fusion(bf16[256,1,8,128]{3,0,2,1:T(8,128)(2,1)S(1)} %get-tuple-element.213, bf16[2,4096,128]{2,1,0:T(8,128)(2,1)} %get-tuple-element.212, s32[]{:T(128)S(6)} %select_n.37), kind=kOutput, calls=%fused_computation.1.clone.1 | convolution fusion | flops 541063168 | bytes 9183236 | tf_op jit(solution)/shard_map/while/body/eval_jaxpr/xlpm,vlm->lpxv/dot_general | solution.py:71
  247.2 0.0 copy-start.1
  247.2 4.6 %fusion.41 = f32[1,8,256,128]{3,2,1,0:T(8,128)S(1)} fusion(f32[1024,256,8]{1,0,2:T(8,128)} %get-tuple-element.184, f32[8,256]{1,0:T(8,128)S(1)} %bitcast.126, f32[1,8,256,128]{3,2,1,0:T(8,128)S(1)} %get-tuple-element.200, f32[8,256]{1,0:T(8,128)S(1)} %get-tuple-element.185, bf16[2,4096,128]{2,1,0:T(8,128)(2,1)} %get-tuple-element.212, s32[]{:T(128)S(6)} %add.51, ...), kind=kOutput, calls=%fused_computation.10.clone.1 | convolution fusion | flops 543686656 | bytes 10764296 | tf_op jit(solution)/shard_map/while/body/eval_jaxpr/ipuo,oit->iput/dot_general | solution.py:83
  251.8 1.3 copy-done.1
  253.1 1.4 fusion.40
  254.5 5.4 %bitcast_reduce_fusion.2 = (f32[8,256]{1,0:T(8,128)S(1)}, f32[1024,256,8]{1,0,2:T(8,128)}) fusion(bf16[256,1,8,128]{3,0,2,1:T(8,128)(2,1)S(1)} %get-tuple-element.213, bf16[2,4096,128]{2,1,0:T(8,128)(2,1)} %get-tuple-element.212, s32[]{:T(128)S(6)} %select_n.37), kind=kOutput, calls=%fused_computation.1.clone.1 | convolution fusion | flops 541063168 | bytes 9183236 | tf_op jit(solution)/shard_map/while/body/eval_jaxpr/xlpm,vlm->lpxv/dot_general | solution.py:71
  259.9 0.0 copy-start.1
  259.9 4.6 %fusion.41 = f32[1,8,256,128]{3,2,1,0:T(8,128)S(1)} fusion(f32[1024,256,8]{1,0,2:T(8,128)} %get-tuple-element.184, f32[8,256]{1,0:T(8,128)S(1)} %bitcast.126, f32[1,8,256,128]{3,2,1,0:T(8,128)S(1)} %get-tuple-element.200, f32[8,256]{1,0:T(8,128)S(1)} %get-tuple-element.185, bf16[2,4096,128]{2,1,0:T(8,128)(2,1)} %get-tuple-element.212, s32[]{:T(128)S(6)} %add.51, ...), kind=kOutput, calls=%fused_computation.10.clone.1 | convolution fusion | flops 543686656 | bytes 10764296 | tf_op jit(solution)/shard_map/while/body/eval_jaxpr/ipuo,oit->iput/dot_general | solution.py:83
  264.6 1.3 copy-done.1
  265.9 1.4 fusion.40
  267.3 0.3 copy.17
  267.6 0.1 divide_convert_fusion
  267.7 5.8 %convolution_convert_fusion = bf16[256,4096]{1,0:T(8,128)(2,1)S(1)} fusion(bf16[256,1024]{0,1:T(8,128)(2,1)S(1)} %bitcast.129, bf16[1024,4096]{1,0:T(8,128)(2,1)} %param.15), kind=kOutput, calls=%fused_computation.22 | convolution fusion | flops 2148532224 | bytes 11010048 | tf_op jit(solution)/shard_map/dot_general | solution.py:112
  273.5 30.9 %all_to_all.5 = bf16[8,32,4096]{2,1,0:T(8,128)(2,1)S(1)} all-to-all(bf16[8,32,4096]{2,1,0:T(8,128)(2,1)S(1)} %bitcast.124), channel_id=1, replica_groups=mesh['rep'=32,'tp'=8] {'tp'}, dimensions={0} | all-to-all | bytes 4194304 | tf_op jit(solution)/shard_map/all_to_all | solution.py:35
  304.4 1.1 reduce_sum.35
  (12 shorter events, 0.1 us)
Async XLA Ops:
  6.5 125.8 %copy-start = (bf16[256,128]{1,0:T(8,128)(2,1)S(1)}, bf16[256,128]{1,0:T(8,128)(2,1)}, u32[]{:S(2)}) copy-start(bf16[256,128]{1,0:T(8,128)(2,1)} %param.10) | copy-start | bytes 196612
  6.5 125.7 %copy-start.3 = (s32[1,2]{1,0:T(1,128)S(1)}, s32[1,2]{1,0:T(1,128)}, u32[]{:S(2)}) copy-start(s32[1,2]{1,0:T(1,128)} %param.14) | copy-start | bytes 28
  6.5 126.1 %copy-start.2 = (bf16[256,128]{1,0:T(8,128)(2,1)S(1)}, bf16[256,128]{1,0:T(8,128)(2,1)}, u32[]{:S(2)}) copy-start(bf16[256,128]{1,0:T(8,128)(2,1)} %param.11) | copy-start | bytes 196612
  6.5 123.3 %reduce-scatter.2.cloned.1.call-start = ((), (), s32[]{:S(2)}) async-start(), calls=%async_computation.2 | async-start | bytes 2162688 | tf_op jit(solution)/shard_map/reduce_scatter | solution.py:24
  8.8 207.4 %all-gather.2.cloned.1.call-start = ((), (), s32[]{:S(2)}) async-start(), calls=%async_computation.3 | async-start | bytes 2162688 | tf_op jit(solution)/shard_map/all_gather | solution.py:25
  221.6 5.9 %copy-start.1 = (f32[1024,256,8]{1,0,2:T(8,128)S(1)}, f32[1024,256,8]{1,0,2:T(8,128)}, u32[]{:S(2)}) copy-start(f32[1024,256,8]{1,0,2:T(8,128)} %get-tuple-element.184) | copy-start | bytes 25165828 | tf_op jit(solution)/shard_map/while
  234.4 5.9 %copy-start.1 = (f32[1024,256,8]{1,0,2:T(8,128)S(1)}, f32[1024,256,8]{1,0,2:T(8,128)}, u32[]{:S(2)}) copy-start(f32[1024,256,8]{1,0,2:T(8,128)} %get-tuple-element.184) | copy-start | bytes 25165828 | tf_op jit(solution)/shard_map/while
  247.2 5.9 %copy-start.1 = (f32[1024,256,8]{1,0,2:T(8,128)S(1)}, f32[1024,256,8]{1,0,2:T(8,128)}, u32[]{:S(2)}) copy-start(f32[1024,256,8]{1,0,2:T(8,128)} %get-tuple-element.184) | copy-start | bytes 25165828 | tf_op jit(solution)/shard_map/while
  259.9 5.9 %copy-start.1 = (f32[1024,256,8]{1,0,2:T(8,128)S(1)}, f32[1024,256,8]{1,0,2:T(8,128)}, u32[]{:S(2)}) copy-start(f32[1024,256,8]{1,0,2:T(8,128)} %get-tuple-element.184) | copy-start | bytes 25165828 | tf_op jit(solution)/shard_map/while
Sparse Core Ops, SparseCore 0:
  11.5 118.2 reduce-scatter.1
  132.6 83.5 all-gather.1
where the time goes:
time: 313 us; the launch traced here: 312 us
  waiting for transfers between devices  204 us (65%)
  matrix products  46.6 us (15%)
  blocking collectives  30.9 us (10%)
  between operations  14.2 us (5%)
  other arithmetic  8.46 us (3%)
  local copies, waits for them, and re-layouts  8.3 us (3%)
    reduce_scatter x1, waiting for transfers between devices, broadcast_by_parts(): own = lax.psum_scatter(padded, axis, scatter_dimension=0, tiled=True)  121 us
    all_gather x1, waiting for transfers between devices, broadcast_by_parts(): lax.all_gather(own, axis, axis=0, tiled=True)[:len(lines)]  82.6 us
    all_to_all x1, blocking collectives, summed_on_arrival(): tiles = lax.all_to_all(split_up(shard, dim, count), axis, 0, 0, tiled=True)  30.9 us
    dot_general x4, matrix products, absorb(): jnp.einsum('xlpm,vlm->lpxv', query_grid, block_keys.reshape(block_width,...  21.7 us
    dot_general x4, matrix products, absorb(): jnp.einsum('ipuo,oit->iput', block_expo.astype(jnp.bfloat16), block_value...  18.4 us
  transfers between devices with their start and end apart: 2, of which 2 were waited for; matrix products, arithmetic and copies ran while one was open for 1% of the time, Pallas kernels for 0%

commit v1 on v0

--- a/solution.py
+++ b/solution.py
@@ -22,7 +22,9 @@
     )
     padded = padded_to(lines, lax.axis_size(axis))
     own = lax.psum_scatter(padded, axis, scatter_dimension=0, tiled=True)
-    return lax.all_gather(own, axis, axis=0, tiled=True)[: len(lines)].reshape(shard.shape)
+    return jnp.concatenate(
+        lax.all_to_all(jnp.stack([own] * lax.axis_size(axis)), axis, 0, 0), axis=0
+    )[: len(lines)].reshape(shard.shape)
 
 
 def split_up(shard, dim, count):

time: 313 us -> 293 us (0.936)
  waiting for transfers between devices: 204 us -> 170 us
  starting transfers between devices: 0.04 us -> 11.8 us
    all_gather x1 -> x0, waiting for transfers between devices: 82.6 us -> none  [broadcast_by_parts(): lax.all_gather(own, axis, axis=0, tiled=True)[:len(lines)]]
    all_to_all x0 -> x1, waiting for transfers between devices: none -> 49.2 us  [broadcast_by_parts(): lax.all_to_all(jnp.stack([own] * lax.axis_size(axis)), axis, 0, 0)]
    all_to_all x0 -> x1, starting transfers between devices: none -> 11.7 us  [broadcast_by_parts(): lax.all_to_all(jnp.stack([own] * lax.axis_size(axis)), axis, 0, 0)]
where the time goes in v1:
time: 293 us; the launch traced here: 291 us
  waiting for transfers between devices  170 us (58%)
  matrix products  46.6 us (16%)
  blocking collectives  30.4 us (10%)
  between operations  14.2 us (5%)
  starting transfers between devices  11.8 us (4%)
  local copies, waits for them, and re-layouts  8.87 us (3%)
  other arithmetic  8.46 us (3%)
    reduce_scatter x1, waiting for transfers between devices, broadcast_by_parts(): own = lax.psum_scatter(padded, axis, scatter_dimension=0, tiled=True)  121 us
    all_to_all x1, waiting for transfers between devices, broadcast_by_parts(): lax.all_to_all(jnp.stack([own] * lax.axis_size(axis)), axis, 0, 0)  49.2 us
    all_to_all x1, blocking collectives, summed_on_arrival(): tiles = lax.all_to_all(split_up(shard, dim, count), axis, 0, 0, tiled=True)  30.4 us
    dot_general x4, matrix products, absorb(): jnp.einsum('xlpm,vlm->lpxv', query_grid, block_keys.reshape(block_width,...  21.7 us
    dot_general x4, matrix products, absorb(): jnp.einsum('ipuo,oit->iput', block_expo.astype(jnp.bfloat16), block_value...  18.4 us
    all_to_all x1, starting transfers between devices, broadcast_by_parts(): lax.all_to_all(jnp.stack([own] * lax.axis_size(axis)), axis, 0, 0)  11.7 us
  transfers between devices with their start and end apart: 2, of which 2 were waited for; matrix products, arithmetic and copies ran while one was open for 1% of the time, Pallas kernels for 0%

profile of v1, /device:TPU:1, one launch (start us, length us, event | category | flops | bytes accessed | tf_op | source)
XLA Modules:
  0.0 290.6 jit_solution(16596586488940000652)
XLA Ops:
  6.5 0.0 copy-start
  6.5 0.0 copy-start.2
  6.5 0.0 copy-start.4
  6.5 0.0 copy-start.3
  6.5 0.0 reduce-scatter.2.cloned.1.call-start
  7.3 1.5 broadcast_select_fusion
  8.8 0.0 reduce-scatter.2.cloned.1.call-update
  8.8 121.0 %reduce-scatter.2.cloned.1.call-done = bf16[256,128]{1,0:T(8,128)(2,1)} async-done(((bf16[8192,128]{1,0:T(8,128)(2,1)}), bf16[256,128]{1,0:T(8,128)(2,1)}) %reduce-scatter.2.cloned.1.call-update) | async-done | bytes 65552 | tf_op jit(solution)/shard_map/reduce_scatter | solution.py:24
  129.8 2.7 stack.2
  132.5 11.7 %all-to-all-start = ((bf16[32,256,128]{2,1,0:T(8,128)(2,1)}), bf16[32,256,128]{2,1,0:T(8,128)(2,1)}, u32[]{:S(2)}, u32[]{:S(2)}) async-start(bf16[32,256,128]{2,1,0:T(8,128)(2,1)} %stack.2), calls=%async_computation.1 | async-start | bytes 4194304 | tf_op jit(solution)/shard_map/all_to_all | solution.py:26
  144.2 0.0 copy-done.2
  144.2 0.2 copy.15
  144.4 0.1 copy.22
  144.5 0.0 copy-done.4
  144.6 0.1 iota_compare_fusion
  144.6 0.0 copy-done
  144.6 0.3 fusion.29
  145.0 0.0 copy-done.3
  145.0 0.4 convolution_bitcast_fusion
  145.3 0.1 copy.14
  145.4 0.3 copy.16
  145.7 0.2 fusion.24
  145.9 49.2 %all-to-all-done = bf16[32,256,128]{2,1,0:T(8,128)(2,1)} async-done(((bf16[32,256,128]{2,1,0:T(8,128)(2,1)}), bf16[32,256,128]{2,1,0:T(8,128)(2,1)}, u32[]{:S(2)}, u32[]{:S(2)}) %all-to-all-start) | async-done | bytes 2097184 | tf_op jit(solution)/shard_map/all_to_all | solution.py:26
  195.0 51.1 %while.17 = (s32[]{:T(128)}, f32[1,8,256]{2,1,0:T(8,128)S(1)}, f32[1,8,256]{2,1,0:T(8,128)S(1)}, f32[1,8,256,128]{3,2,1,0:T(8,128)S(1)}, bf16[2,4096,128]{2,1,0:...) while((s32[]{:T(128)}, f32[1,8,256]{2,1,0:T(8,128)S(1)}, ...), condition=%wide.region_6.7_spmd, body=%wide.region_3.6_spmd.sunk | while | flops 1091049472 | bytes 61997260 | solution.py:104
  195.0 5.4 %bitcast_reduce_fusion.2 = (f32[8,256]{1,0:T(8,128)S(1)}, f32[1024,256,8]{1,0,2:T(8,128)}) fusion(bf16[256,1,8,128]{3,0,2,1:T(8,128)(2,1)S(1)} %get-tuple-element.213, bf16[2,4096,128]{2,1,0:T(8,128)(2,1)} %get-tuple-element.212, s32[]{:T(128)S(6)} %select_n.37), kind=kOutput, calls=%fused_computation.1.clone.1 | convolution fusion | flops 541063168 | bytes 9183236 | tf_op jit(solution)/shard_map/while/body/eval_jaxpr/xlpm,vlm->lpxv/dot_general | solution.py:73
  200.5 0.0 copy-start.1
  200.5 4.6 %fusion.41 = f32[1,8,256,128]{3,2,1,0:T(8,128)S(1)} fusion(f32[1024,256,8]{1,0,2:T(8,128)} %get-tuple-element.184, f32[8,256]{1,0:T(8,128)S(1)} %bitcast.126, f32[1,8,256,128]{3,2,1,0:T(8,128)S(1)} %get-tuple-element.200, f32[8,256]{1,0:T(8,128)S(1)} %get-tuple-element.185, bf16[2,4096,128]{2,1,0:T(8,128)(2,1)} %get-tuple-element.212, s32[]{:T(128)S(6)} %add.51, ...), kind=kOutput, calls=%fused_computation.10.clone.1 | convolution fusion | flops 543686656 | bytes 10764296 | tf_op jit(solution)/shard_map/while/body/eval_jaxpr/ipuo,oit->iput/dot_general | solution.py:85
  205.1 1.3 copy-done.1
  206.4 1.4 fusion.40
  207.8 5.4 %bitcast_reduce_fusion.2 = (f32[8,256]{1,0:T(8,128)S(1)}, f32[1024,256,8]{1,0,2:T(8,128)}) fusion(bf16[256,1,8,128]{3,0,2,1:T(8,128)(2,1)S(1)} %get-tuple-element.213, bf16[2,4096,128]{2,1,0:T(8,128)(2,1)} %get-tuple-element.212, s32[]{:T(128)S(6)} %select_n.37), kind=kOutput, calls=%fused_computation.1.clone.1 | convolution fusion | flops 541063168 | bytes 9183236 | tf_op jit(solution)/shard_map/while/body/eval_jaxpr/xlpm,vlm->lpxv/dot_general | solution.py:73
  213.3 0.0 copy-start.1
  213.3 4.6 %fusion.41 = f32[1,8,256,128]{3,2,1,0:T(8,128)S(1)} fusion(f32[1024,256,8]{1,0,2:T(8,128)} %get-tuple-element.184, f32[8,256]{1,0:T(8,128)S(1)} %bitcast.126, f32[1,8,256,128]{3,2,1,0:T(8,128)S(1)} %get-tuple-element.200, f32[8,256]{1,0:T(8,128)S(1)} %get-tuple-element.185, bf16[2,4096,128]{2,1,0:T(8,128)(2,1)} %get-tuple-element.212, s32[]{:T(128)S(6)} %add.51, ...), kind=kOutput, calls=%fused_computation.10.clone.1 | convolution fusion | flops 543686656 | bytes 10764296 | tf_op jit(solution)/shard_map/while/body/eval_jaxpr/ipuo,oit->iput/dot_general | solution.py:85
  217.9 1.3 copy-done.1
  219.2 1.4 fusion.40
  220.6 5.4 %bitcast_reduce_fusion.2 = (f32[8,256]{1,0:T(8,128)S(1)}, f32[1024,256,8]{1,0,2:T(8,128)}) fusion(bf16[256,1,8,128]{3,0,2,1:T(8,128)(2,1)S(1)} %get-tuple-element.213, bf16[2,4096,128]{2,1,0:T(8,128)(2,1)} %get-tuple-element.212, s32[]{:T(128)S(6)} %select_n.37), kind=kOutput, calls=%fused_computation.1.clone.1 | convolution fusion | flops 541063168 | bytes 9183236 | tf_op jit(solution)/shard_map/while/body/eval_jaxpr/xlpm,vlm->lpxv/dot_general | solution.py:73
  226.0 0.0 copy-start.1
  226.0 4.6 %fusion.41 = f32[1,8,256,128]{3,2,1,0:T(8,128)S(1)} fusion(f32[1024,256,8]{1,0,2:T(8,128)} %get-tuple-element.184, f32[8,256]{1,0:T(8,128)S(1)} %bitcast.126, f32[1,8,256,128]{3,2,1,0:T(8,128)S(1)} %get-tuple-element.200, f32[8,256]{1,0:T(8,128)S(1)} %get-tuple-element.185, bf16[2,4096,128]{2,1,0:T(8,128)(2,1)} %get-tuple-element.212, s32[]{:T(128)S(6)} %add.51, ...), kind=kOutput, calls=%fused_computation.10.clone.1 | convolution fusion | flops 543686656 | bytes 10764296 | tf_op jit(solution)/shard_map/while/body/eval_jaxpr/ipuo,oit->iput/dot_general | solution.py:85
  230.7 1.3 copy-done.1
  232.0 1.4 fusion.40
  233.4 5.4 %bitcast_reduce_fusion.2 = (f32[8,256]{1,0:T(8,128)S(1)}, f32[1024,256,8]{1,0,2:T(8,128)}) fusion(bf16[256,1,8,128]{3,0,2,1:T(8,128)(2,1)S(1)} %get-tuple-element.213, bf16[2,4096,128]{2,1,0:T(8,128)(2,1)} %get-tuple-element.212, s32[]{:T(128)S(6)} %select_n.37), kind=kOutput, calls=%fused_computation.1.clone.1 | convolution fusion | flops 541063168 | bytes 9183236 | tf_op jit(solution)/shard_map/while/body/eval_jaxpr/xlpm,vlm->lpxv/dot_general | solution.py:73
  238.8 4.6 %fusion.41 = f32[1,8,256,128]{3,2,1,0:T(8,128)S(1)} fusion(f32[1024,256,8]{1,0,2:T(8,128)} %get-tuple-element.184, f32[8,256]{1,0:T(8,128)S(1)} %bitcast.126, f32[1,8,256,128]{3,2,1,0:T(8,128)S(1)} %get-tuple-element.200, f32[8,256]{1,0:T(8,128)S(1)} %get-tuple-element.185, bf16[2,4096,128]{2,1,0:T(8,128)(2,1)} %get-tuple-element.212, s32[]{:T(128)S(6)} %add.51, ...), kind=kOutput, calls=%fused_computation.10.clone.1 | convolution fusion | flops 543686656 | bytes 10764296 | tf_op jit(solution)/shard_map/while/body/eval_jaxpr/ipuo,oit->iput/dot_general | solution.py:85
  243.4 1.3 copy-done.1
  244.7 1.4 fusion.40
  246.2 0.3 copy.17
  246.5 0.1 divide_convert_fusion
  246.6 5.8 %convolution_convert_fusion = bf16[256,4096]{1,0:T(8,128)(2,1)S(1)} fusion(bf16[256,1024]{0,1:T(8,128)(2,1)S(1)} %bitcast.128, bf16[1024,4096]{1,0:T(8,128)(2,1)} %param.15), kind=kOutput, calls=%fused_computation.22 | convolution fusion | flops 2148532224 | bytes 11010048 | tf_op jit(solution)/shard_map/dot_general | solution.py:114
  252.4 30.4 %all_to_all.10 = bf16[8,32,4096]{2,1,0:T(8,128)(2,1)S(1)} all-to-all(bf16[8,32,4096]{2,1,0:T(8,128)(2,1)S(1)} %bitcast.124), channel_id=1, replica_groups=mesh['rep'=32,'tp'=8] {'tp'}, dimensions={0} | all-to-all | bytes 4194304 | tf_op jit(solution)/shard_map/all_to_all | solution.py:37
  282.7 1.1 reduce_sum.35
  (13 shorter events, 0.1 us)
Async XLA Ops:
  6.5 138.1 %copy-start = (bf16[256,128]{1,0:T(8,128)(2,1)S(1)}, bf16[256,128]{1,0:T(8,128)(2,1)}, u32[]{:S(2)}) copy-start(bf16[256,128]{1,0:T(8,128)(2,1)} %param.10) | copy-start | bytes 196612
  6.5 137.7 %copy-start.2 = (bf16[256,1024]{1,0:T(8,128)(2,1)S(1)}, bf16[256,1024]{1,0:T(8,128)(2,1)}, u32[]{:S(2)}) copy-start(bf16[256,1024]{1,0:T(8,128)(2,1)} %param.9) | copy-start | bytes 1572868
  6.5 138.0 %copy-start.4 = (s32[1,2]{1,0:T(1,128)S(1)}, s32[1,2]{1,0:T(1,128)}, u32[]{:S(2)}) copy-start(s32[1,2]{1,0:T(1,128)} %param.14) | copy-start | bytes 28
  6.5 138.4 %copy-start.3 = (bf16[256,128]{1,0:T(8,128)(2,1)S(1)}, bf16[256,128]{1,0:T(8,128)(2,1)}, u32[]{:S(2)}) copy-start(bf16[256,128]{1,0:T(8,128)(2,1)} %param.11) | copy-start | bytes 196612
  6.5 123.3 %reduce-scatter.2.cloned.1.call-start = ((), (), s32[]{:S(2)}) async-start(), calls=%async_computation.3 | async-start | bytes 2162688 | tf_op jit(solution)/shard_map/reduce_scatter | solution.py:24
  132.5 62.6 %all-to-all-start = ((bf16[32,256,128]{2,1,0:T(8,128)(2,1)}), bf16[32,256,128]{2,1,0:T(8,128)(2,1)}, u32[]{:S(2)}, u32[]{:S(2)}) async-start(bf16[32,256,128]{2,1,0:T(8,128)(2,1)} %stack.2), calls=%async_computation.1 | async-start | bytes 4194304 | tf_op jit(solution)/shard_map/all_to_all | solution.py:26
  200.5 5.9 %copy-start.1 = (f32[1024,256,8]{1,0,2:T(8,128)S(1)}, f32[1024,256,8]{1,0,2:T(8,128)}, u32[]{:S(2)}) copy-start(f32[1024,256,8]{1,0,2:T(8,128)} %get-tuple-element.184) | copy-start | bytes 25165828 | tf_op jit(solution)/shard_map/while
  213.3 5.9 %copy-start.1 = (f32[1024,256,8]{1,0,2:T(8,128)S(1)}, f32[1024,256,8]{1,0,2:T(8,128)}, u32[]{:S(2)}) copy-start(f32[1024,256,8]{1,0,2:T(8,128)} %get-tuple-element.184) | copy-start | bytes 25165828 | tf_op jit(solution)/shard_map/while
  226.0 5.9 %copy-start.1 = (f32[1024,256,8]{1,0,2:T(8,128)S(1)}, f32[1024,256,8]{1,0,2:T(8,128)}, u32[]{:S(2)}) copy-start(f32[1024,256,8]{1,0,2:T(8,128)} %get-tuple-element.184) | copy-start | bytes 25165828 | tf_op jit(solution)/shard_map/while
  238.8 5.9 %copy-start.1 = (f32[1024,256,8]{1,0,2:T(8,128)S(1)}, f32[1024,256,8]{1,0,2:T(8,128)}, u32[]{:S(2)}) copy-start(f32[1024,256,8]{1,0,2:T(8,128)} %get-tuple-element.184) | copy-start | bytes 25165828 | tf_op jit(solution)/shard_map/while
Sparse Core Ops, SparseCore 0:
  11.5 118.2 reduce-scatter.1
